TPU v7x, 32 devices: a whole 2x2x4 slice. The times are simulated.
32 devices in a mesh: seq: 16 (over z, y, x), head: 2 (over core).
Axes of the slice: x: 2, y: 2, z: 4, core: 2. Of those that a mesh axis runs over, the one named last changes fastest.
Arguments:
- tokens: bfloat16 [8192, 3584], P('seq', 'head'), may hold values from -6 to 6
- pre_gain: float32 [3584], replicated, may hold values from 0.5 to 1.5
- query_weight: bfloat16 [3584, 2048], P(None, 'head'), may hold values from -0.375 to 0.375
- key_weight: bfloat16 [3584, 1024], P(None, 'head'), may hold values from -0.375 to 0.375
- value_weight: bfloat16 [3584, 1024], P(None, 'head'), may hold values from -0.09375 to 0.09375
- out_weight: bfloat16 [2048, 3584], P('head'), may hold values from -0.5 to 0.5
- post_gain: float32 [3584], P('head'), may hold values from 0.5 to 1.5
Outputs:
- layer_out: bfloat16 [8192, 3584], P('seq', 'head')
All inputs are finite; a program needn't handle non-finite values.
Results may differ from a plain program's by a relative error of at most 0.013.
The roundings to bfloat16 on the way count: a program that leaves them out, or rounds other values in their place, can miss the bound.
Values may be sent and summed in bfloat16 or wider, within the bound.
A program may use at most 192 MiB of HBM per device.

v0:
```python
import functools
import math

import jax
import jax.numpy as jnp
from jax import lax
from jax.experimental import pallas as pl
from jax.experimental.pallas import tpu as pltpu
from jax.sharding import PartitionSpec as P

HD = 256
WINDOW = 4096

softcap_limit = 50.0
rope_base = 10000.0
norm_epsilon = 1e-06

ROW_TILE = 256

X_KV, X_Q, Z_NEAR, Z_FAR, Y_NEAR, Y_FAR, X_OUT, MESSAGES = 0, 1, 2, 4, 6, 8, 10, 11


def attention_kernel(
    blocks, rows, q_ref, kv_ref, out_ref,
    held, queries, total, mass, leaving, landed, send_sems, recv_sems,
):
    group = 2 * 2
    me = lax.axis_index("seq")
    x = me % 2
    y = (me // 2) % 2
    x_mate = me + 1 - 2 * x
    y_mate = me + 2 - 4 * y
    z_next = me + group
    has_next = z_next < blocks
    has_prev = me >= group

    def copy(message, src, dst, device):
        return pltpu.make_async_remote_copy(
            src_ref=src,
            dst_ref=dst,
            send_sem=send_sems.at[message],
            recv_sem=recv_sems.at[message],
            device_id={"seq": device},
            device_id_type=pl.DeviceIdType.MESH,
        )

    barrier = pltpu.get_barrier_semaphore()

    def greet(device):
        pl.semaphore_signal(
            barrier, inc=1, device_id={"seq": device}, device_id_type=pl.DeviceIdType.MESH
        )

    greet(x_mate)
    greet(y_mate)
    pl.when(has_next)(lambda: greet(z_next))
    pl.when(has_prev)(lambda: greet(me - group))
    pl.semaphore_wait(barrier, 2 + has_next.astype(jnp.int32) + has_prev.astype(jnp.int32))

    own_kv = kv_ref.at[x]
    send_kv = copy(X_KV, kv_ref.at[1 - x], held.at[0, 1], x_mate)
    send_q = copy(X_Q, q_ref.at[1 - x], queries.at[1], x_mate)
    near = lambda r: own_kv if r == 0 else held.at[0, 1]
    z_near = [copy(Z_NEAR + r, near(r), held.at[2, r], z_next) for r in range(2)]
    z_far = [copy(Z_FAR + r, held.at[2, r], held.at[4, r], z_next) for r in range(2)]
    y_up_near = [copy(Y_NEAR + r, near(r), held.at[1, r], y_mate) for r in range(2)]
    y_up_far = [copy(Y_FAR + r, held.at[2, r], held.at[3, r], y_mate) for r in range(2)]
    y_down_near = [copy(Y_NEAR + r, held.at[2, r], held.at[1, r], y_mate) for r in range(2)]
    y_down_far = [copy(Y_FAR + r, held.at[4, r], held.at[3, r], y_mate) for r in range(2)]

    first_row = y == 0
    second_row = y == 1

    send_kv.start()
    pl.when(has_next)(lambda: z_near[0].start())
    pl.when(first_row)(lambda: y_up_near[0].start())
    send_q.start()

    queries[0] = q_ref[x]
    total[...] = jnp.zeros_like(total)
    mass[...] = jnp.zeros_like(mass)

    tiles_per_side = 2 * rows // ROW_TILE
    tiles_per_head = rows // ROW_TILE
    inner = 1.0 / (math.sqrt(HD) * softcap_limit)
    outer = softcap_limit / math.log(2.0)

    def attend(block, first, last, distances):
        def tile(t, carry):
            side = t // tiles_per_side
            within = t % tiles_per_side
            head = within // tiles_per_head
            start = pl.multiple_of((within % tiles_per_head) * ROW_TILE, ROW_TILE)
            q = queries[side, head, pl.ds(start, ROW_TILE), :]
            scores = lax.dot_general(
                q, block[0], (((1,), (1,)), ((), ())), preferred_element_type=jnp.float32
            )
            weights = jnp.exp2(outer * jnp.tanh(scores * inner))
            if distances is not None:
                distance = jnp.where(side == 0, distances[0], distances[1])
                offset = (
                    distance * rows
                    + start
                    + lax.broadcasted_iota(jnp.int32, weights.shape, 0)
                    - lax.broadcasted_iota(jnp.int32, weights.shape, 1)
                )
                weights = jnp.where((offset >= 0) & (offset < WINDOW), weights, 0.0)
            part = weights[:, :128]
            for k in range(1, rows // 128):
                part = part + weights[:, k * 128 : (k + 1) * 128]
            mass[side, head, pl.ds(start, ROW_TILE), :] += part
            total[side, head, pl.ds(start, ROW_TILE), :] += jnp.dot(
                weights.astype(jnp.bfloat16), block[1], preferred_element_type=jnp.float32
            )
            return carry

        lax.fori_loop(first, last, tile, 0)

    both = 2 * tiles_per_side
    def ahead(d, r, side):
        if side == r:
            return jnp.int32(2 * d)
        return 2 * d + (2 * x - 1 if side == 0 else 1 - 2 * x)

    def edge(d, r):
        return (ahead(d, r, 0), ahead(d, r, 1))

    reach = WINDOW // rows

    def bounds(d, r):
        low, high = edge(d, r)
        fits = lambda e: (e >= 0) & (e <= reach)
        first = jnp.where(fits(low), 0, tiles_per_side)
        last = jnp.where(fits(high), both, tiles_per_side)
        return first, last

    attend(own_kv, 0, tiles_per_side, edge(0, 0))

    send_kv.wait_recv()
    pl.when(has_next)(lambda: z_near[1].start())
    pl.when(first_row)(lambda: y_up_near[1].start())

    def forward_near(r):
        z_near[r].wait_recv()
        pl.when(has_next)(lambda: z_far[r].start())
        pl.when(first_row)(lambda: y_up_far[r].start())
        pl.when(second_row)(lambda: y_down_near[r].start())

    pl.when(has_prev)(lambda: forward_near(0))

    send_q.wait_recv()
    first, last = bounds(0, 0)
    attend(own_kv, tiles_per_side, last, edge(0, 0))
    first, last = bounds(0, 1)
    attend(held.at[0, 1], first, last, edge(0, 1))

    has_far = me >= 2 * group

    @pl.when(has_prev)
    def _():
        attend(held.at[2, 0], 0, both, None)

    @pl.when(me >= 2)
    def _():
        y_up_near[0].wait_recv()
        attend(held.at[1, 0], 0, both, None)

    @pl.when(has_prev)
    def _():
        forward_near(1)
        attend(held.at[2, 1], 0, both, None)

    def far(r):
        z_far[r].wait_recv()
        pl.when(second_row)(lambda: y_down_far[r].start())
        first, last = bounds(4, r)
        attend(held.at[4, r], first, last, edge(4, r))

    pl.when(has_far)(lambda: far(0))

    @pl.when(me >= 2)
    def _():
        y_up_near[1].wait_recv()
        attend(held.at[1, 1], 0, both, None)

    @pl.when(me >= 6)
    def _():
        y_up_far[0].wait_recv()
        attend(held.at[3, 0], 0, both, None)

    pl.when(has_far)(lambda: far(1))

    @pl.when(me >= 6)
    def _():
        y_up_far[1].wait_recv()
        attend(held.at[3, 1], 0, both, None)

    def finished(side, head):
        weight = jnp.sum(mass[side, head], axis=-1, keepdims=True)
        return (total[side, head] / weight).astype(jnp.bfloat16)

    for head in range(2):
        leaving[head] = finished(1, head)
    send_out = copy(X_OUT, leaving, landed, x_mate)
    for head in range(2):
        at = pl.multiple_of((2 * x + head) * HD, HD)
        value = finished(0, head)
        out_ref[:, pl.ds(at, HD)] = value
        if head == 0:
            send_out.start()
    send_out.wait_recv()
    for head in range(2):
        at = pl.multiple_of((2 * (1 - x) + head) * HD, HD)
        out_ref[:, pl.ds(at, HD)] = landed[head]

    send_kv.wait_send()
    send_q.wait_send()
    send_out.wait_send()
    for r in range(2):
        pl.when(has_next)(lambda: z_near[r].wait_send())
        pl.when(has_next & has_prev)(lambda: z_far[r].wait_send())
        pl.when(first_row)(lambda: y_up_near[r].wait_send())
        pl.when(first_row & has_prev)(lambda: y_up_far[r].wait_send())
        pl.when(second_row & has_prev)(lambda: y_down_near[r].wait_send())
        pl.when(second_row & has_far)(lambda: y_down_far[r].wait_send())


def attention(q, kv, blocks):
    rows = q.shape[2]
    half = (2, rows, HD)
    vmem = pl.BlockSpec(memory_space=pltpu.VMEM)
    return pl.pallas_call(
        functools.partial(attention_kernel, blocks, rows),
        out_shape=jax.ShapeDtypeStruct((rows, 4 * HD), jnp.bfloat16),
        in_specs=[vmem, vmem],
        out_specs=vmem,
        scratch_shapes=[
            pltpu.VMEM((5, 2) + half, jnp.bfloat16),
            pltpu.VMEM((2,) + half, jnp.bfloat16),
            pltpu.VMEM((2,) + half, jnp.float32),
            pltpu.VMEM((2, 2, rows, 128), jnp.float32),
            pltpu.VMEM(half, jnp.bfloat16),
            pltpu.VMEM(half, jnp.bfloat16),
            pltpu.SemaphoreType.DMA((MESSAGES,)),
            pltpu.SemaphoreType.DMA((MESSAGES,)),
        ],
        compiler_params=pltpu.CompilerParams(
            collective_id=0, has_side_effects=True, vmem_limit_bytes=48 * 1024 * 1024
        ),
    )(q, kv)


def swap_heads(shard):
    return lax.ppermute(shard, "head", [(0, 1), (1, 0)])


def rope_tables(positions):
    midpoint = HD // 2
    frequency = jnp.exp(
        -jnp.log(rope_base) * (2.0 * jnp.arange(midpoint, dtype=jnp.float32) / HD)
    )
    angles = positions.astype(jnp.float32)[:, None] * frequency[None, :]
    return jnp.cos(angles), jnp.sin(angles)


def rotated(head, cosine, sine):
    midpoint = HD // 2
    leading, trailing = head[:, :midpoint], head[:, midpoint:]
    return jnp.concatenate(
        [leading * cosine - trailing * sine, trailing * cosine + leading * sine], axis=-1
    ).astype(jnp.bfloat16)


def local(blocks, tokens, pre_gain, query_weight, key_weight, value_weight, out_weight, post_gain):
    rows, width = tokens.shape
    side = lax.axis_index("head")
    other = swap_heads(tokens)
    full = jnp.where(
        side == 0,
        jnp.concatenate([tokens, other], axis=1),
        jnp.concatenate([other, tokens], axis=1),
    )
    widened = full.astype(jnp.float32)
    scale = lax.rsqrt(
        jnp.sum(widened * widened, axis=-1, keepdims=True) / widened.shape[-1] + norm_epsilon
    )
    normed = (widened * scale * pre_gain).astype(jnp.bfloat16)
    positions = lax.axis_index("seq") * rows + jnp.arange(rows, dtype=jnp.int32)
    cosine, sine = rope_tables(positions)
    project = lambda weight: jnp.dot(normed, weight, preferred_element_type=jnp.float32)
    q_all, k_all, v_all = project(query_weight), project(key_weight), project(value_weight)
    head_of = lambda a, h: a[:, h * HD : (h + 1) * HD]
    q = jnp.stack(
        [
            jnp.stack([rotated(head_of(q_all, 2 * k + g), cosine, sine) for g in range(2)])
            for k in range(2)
        ]
    )
    kv = jnp.stack(
        [
            jnp.stack(
                [rotated(head_of(k_all, k), cosine, sine), head_of(v_all, k).astype(jnp.bfloat16)]
            )
            for k in range(2)
        ]
    )
    attended = attention(q, kv, blocks)
    mine = lax.dynamic_slice_in_dim(out_weight, side * width, width, 1)
    theirs = lax.dynamic_slice_in_dim(out_weight, (1 - side) * width, width, 1)
    given = jnp.dot(attended, theirs, preferred_element_type=jnp.float32).astype(jnp.bfloat16)
    arrived = swap_heads(given)
    kept = jnp.dot(attended, mine, preferred_element_type=jnp.float32)
    share = kept + arrived.astype(jnp.float32)
    squares = jnp.sum(share * share, axis=1, keepdims=True)
    squares = squares + swap_heads(squares)
    inverse_rms = lax.rsqrt(squares / (2 * width) + norm_epsilon)
    return (tokens.astype(jnp.float32) + post_gain * share * inverse_rms).astype(jnp.bfloat16)


def solution(mesh):
    placed = (
        P("seq", "head"),
        P(),
        P(None, "head"),
        P(None, "head"),
        P(None, "head"),
        P("head", None),
        P("head"),
    )
    return jax.shard_map(
        functools.partial(local, mesh.shape["seq"]),
        mesh=mesh,
        in_specs=placed,
        out_specs=P("seq", "head"),
        check_vma=False,
    )
```

profile of v0, /device:TPU:17, one launch (start us, length us, event | category | flops | bytes accessed | tf_op | source)
XLA Modules:
  0.0 128.3 jit_solution(5568206879555744932)
XLA Ops:
  0.0 0.0 copy-start
  0.0 0.0 copy-start.1
  0.0 0.7 collective-permute-start
  0.7 3.7 %collective-permute-done = bf16[512,1792]{1,0:T(8,128)(2,1)} collective-permute-done((bf16[512,1792]{1,0:T(8,128)(2,1)}, bf16[512,1792]{1,0:T(8,128)(2,1)}, u32[]{:S(2)}, u32[]{:S(2)}) %collective-permute-start) | collective-permute-done | bytes 1835040 | tf_op jit(solution)/shard_map/ppermute | solution.py:254
  4.4 4.5 %fusion = f32[512]{0:T(512)S(1)} fusion(bf16[512,1792]{1,0:T(8,128)(2,1)} %param.7, bf16[512,1792]{1,0:T(8,128)(2,1)} %collective-permute-done, pred[]{:T(512)S(6)} %eq.3), kind=kLoop, calls=%fused_computation.2 | loop fusion | flops 22019584 | bytes 3672065 | tf_op jit(solution)/shard_map/reduce_sum | solution.py:285
  9.0 0.0 copy-done
  9.0 0.0 copy-done.1
  9.0 0.0 copy-start.3
  9.0 3.8 %fusion.2 = bf16[512,3584]{1,0:T(8,128)(2,1)S(1)} fusion(f32[3584]{0:T(1024)S(1)} %copy-done.1, f32[512]{0:T(512)S(1)} %add_rsqrt_fusion.1, bf16[512,1792]{1,0:T(8,128)(2,1)S(1)} %copy-done, bf16[512,1792]{1,0:T(8,128)(2,1)} %collective-permute-done, pred[]{:T(512)S(6)} %eq.3), kind=kLoop, calls=%fused_computation.4 | loop fusion | flops 23855104 | bytes 7356417 | tf_op jit(solution)/shard_map/convert_element_type | solution.py:287
  12.8 0.0 copy-done.3
  12.8 0.0 copy-start.4
  12.9 0.0 slice-start
  12.9 2.1 %fusion.75 = f32[512,512]{1,0:T(8,128)S(1)} fusion(bf16[512,3584]{1,0:T(8,128)(2,1)S(1)} %fusion.2, bf16[3584,512]{1,0:T(8,128)(2,1)S(1)} %copy-done.3), kind=kOutput, calls=%fused_computation.92 | convolution fusion | flops 1879048192 | bytes 8388608 | tf_op jit(solution)/shard_map/dot_general | solution.py:290
  14.9 0.0 copy-done.4
  14.9 0.0 slice-start.1
  14.9 2.1 %convolution_convert_fusion = bf16[512,512]{1,0:T(8,128)(2,1)S(1)} fusion(bf16[512,3584]{1,0:T(8,128)(2,1)S(1)} %fusion.2, bf16[3584,512]{1,0:T(8,128)(2,1)S(1)} %copy-done.4), kind=kOutput, calls=%fused_computation.14 | convolution fusion | flops 1879310336 | bytes 7864320 | tf_op jit(solution)/shard_map/dot_general | solution.py:290
  17.0 0.0 slice-done
  17.1 0.2 slice-done.1
  17.3 3.9 %fusion.74 = f32[512,1024]{1,0:T(8,128)S(1)} fusion(bf16[512,3584]{1,0:T(8,128)(2,1)S(1)} %fusion.2, bf16[3584,1024]{1,0:T(8,128)(2,1)S(1)} %bitcast.50), kind=kOutput, calls=%fused_computation.91 | convolution fusion | flops 3758096384 | bytes 13107200 | tf_op jit(solution)/shard_map/dot_general | solution.py:290
  21.2 0.0 slice-start.2
  21.2 1.3 fusion.63
  22.5 1.4 %fusion.71 = (bf16[1,512,128]{2,1,0:T(8,128)(2,1)S(1)}, bf16[1,512,128]{2,1,0:T(8,128)(2,1)S(1)}, bf16[1,512,128]{2,1,0:T(8,128)(2,1)S(1)}, bf16[1,512,128]{2,1,...) fusion(f32[512,1024]{1,0:T(8,128)S(1)} %fusion.74, ...), kind=kLoop, calls=%fused_computation.84 | loop fusion | flops 2162688 | bytes 3148288 | tf_op jit(solution)/shard_map/concatenate | solution.py:269
  23.9 0.1 maximum_bitcast_fusion.2
  24.0 0.0 slice-start.3
  24.0 0.1 pad_maximum_fusion.1.kv_ref
  24.2 0.1 maximum_bitcast_fusion
  24.3 0.1 pad_maximum_fusion.q_ref
  24.4 86.5 %shard_map.73 = bf16[512,1024]{1,0:T(8,128)(2,1)S(1)} custom-call(bf16[2,2,512,256]{3,2,1,0:T(8,128)(2,1)S(1)} %pad_maximum_fusion.q_ref, bf16[2,2,512,256]{3,2,1,0:T(8,128)(2,1)S(1)} %pad_maximum_fusion.1.kv_ref), custom_call_target="tpu_custom_call" | custom-call | tf_op jit(solution)/shard_map/pallas_call | solution.py:232
  110.9 0.0 slice-done.2
  110.9 0.0 slice-done.3
  110.9 3.3 %fusion.9 = bf16[512,1792]{1,0:T(8,128)(2,1)} fusion(bf16[512,1024]{1,0:T(8,128)(2,1)S(1)} %shard_map.73, bf16[1024,3584]{1,0:T(8,128)(2,1)S(1)} %bitcast.52, s32[]{:T(128)S(6)} %select_n.17), kind=kOutput, calls=%fused_computation.13 | convolution fusion | flops 1879965696 | bytes 6553604 | tf_op jit(solution)/shard_map/dot_general | solution.py:310
  114.2 2.4 %collective-permute-start.1 = (bf16[512,1792]{1,0:T(8,128)(2,1)}, bf16[512,1792]{1,0:T(8,128)(2,1)}, u32[]{:S(2)}, u32[]{:S(2)}) collective-permute-start(bf16[512,1792]{1,0:T(8,128)(2,1)} %fusion.9), channel_id=1, source_target_pairs={{0,1},{1,0},{2,3},{3,2},{4,5},{5,4},{6,7},{7,6},{8,9},{9,8},{10,11... | collective-permute-start | bytes 5505032 | tf_op jit(solution)/shard_map/ppermute | solution.py:254
  116.6 0.0 copy-start.2
  116.6 3.8 %collective-permute-done.1 = bf16[512,1792]{1,0:T(8,128)(2,1)} collective-permute-done((bf16[512,1792]{1,0:T(8,128)(2,1)}, bf16[512,1792]{1,0:T(8,128)(2,1)}, u32[]{:S(2)}, u32[]{:S(2)}) %collective-permute-start.1) | collective-permute-done | bytes 1835040 | tf_op jit(solution)/shard_map/ppermute | solution.py:254
  120.4 4.8 %multiply_reduce_fusion = (f32[512]{0:T(512)S(1)}, f32[512,1792]{1,0:T(8,128)S(1)}) fusion(bf16[512,1792]{1,0:T(8,128)(2,1)} %collective-permute-done.1, bf16[512,1024]{1,0:T(8,128)(2,1)S(1)} %shard_map.73, bf16[1024,3584]{1,0:T(8,128)(2,1)} %param.12, s32[]{:T(128)S(6)} %select_n.16), kind=kOutput, calls=%fused_computation.7 | convolution fusion | flops 1882717696 | bytes 10225668 | tf_op jit(solution)/shard_map/dot_general | solution.py:312
  125.1 0.4 collective-permute-start.2
  125.6 0.8 collective-permute-done.2
  126.4 0.0 copy-done.2
  126.4 1.9 %add_convert_fusion = bf16[512,1792]{1,0:T(8,128)(2,1)} fusion(f32[512,1792]{1,0:T(8,128)S(1)} %get-tuple-element.20, bf16[512,1792]{1,0:T(8,128)(2,1)S(1)} %copy-done, f32[512]{0:T(512)S(1)} %bitcast.46, f32[1792]{0:T(1024)S(1)} %copy-done.2), kind=kLoop, calls=%fused_computation.6 | loop fusion | flops 4587520 | bytes 7349248 | tf_op jit(solution)/shard_map/convert_element_type | solution.py:317
  (7 shorter events, 0.1 us)
Async XLA Ops:
  0.0 9.0 %copy-start = (bf16[512,1792]{1,0:T(8,128)(2,1)S(1)}, bf16[512,1792]{1,0:T(8,128)(2,1)}, u32[]{:S(2)}) copy-start(bf16[512,1792]{1,0:T(8,128)(2,1)} %param.7) | copy-start | bytes 5505028
  0.0 9.0 %copy-start.1 = (f32[3584]{0:T(1024)S(1)}, f32[3584]{0:T(1024)}, u32[]{:S(2)}) copy-start(f32[3584]{0:T(1024)} %param.8) | copy-start | bytes 43012
  0.0 4.4 %collective-permute-start = (bf16[512,1792]{1,0:T(8,128)(2,1)}, bf16[512,1792]{1,0:T(8,128)(2,1)}, u32[]{:S(2)}, u32[]{:S(2)}) collective-permute-start(bf16[512,1792]{1,0:T(8,128)(2,1)} %param.7), channel_id=1, source_target_pairs={{0,1},{1,0},{2,3},{3,2},{4,5},{5,4},{6,7},{7,6},{8,9},{9,8},{10,11... | collective-permute-start | bytes 5505032 | tf_op jit(solution)/shard_map/ppermute | solution.py:254
  9.0 3.8 %copy-start.3 = (bf16[3584,512]{1,0:T(8,128)(2,1)S(1)}, bf16[3584,512]{1,0:T(8,128)(2,1)}, u32[]{:S(2)}) copy-start(bf16[3584,512]{1,0:T(8,128)(2,1)} %param.10) | copy-start | bytes 11010052
  12.8 2.1 %copy-start.4 = (bf16[3584,512]{1,0:T(8,128)(2,1)S(1)}, bf16[3584,512]{1,0:T(8,128)(2,1)}, u32[]{:S(2)}) copy-start(bf16[3584,512]{1,0:T(8,128)(2,1)} %param.11) | copy-start | bytes 11010052
  12.9 4.2 %slice-start = ((s8[7340032]{0:T(1024)(128)(4,1)}), s8[4194304]{0:T(1024)(128)(4,1)S(1)}, s32[]{:S(2)}) async-start(s8[7340032]{0:T(1024)(128)(4,1)} %bitcast.49), calls=%async_computation | async-start | bytes 8388608
  14.9 2.3 %slice-start.1 = ((s8[7340032]{0:T(1024)(128)(4,1)}), s8[3145728]{0:T(1024)(128)(4,1)S(1)}, s32[]{:S(2)}) async-start(s8[7340032]{0:T(1024)(128)(4,1)} %bitcast.49), calls=%async_computation.1 | async-start | bytes 6291456
  21.2 89.6 %slice-start.2 = ((s8[7340032]{0:T(1024)(128)(4,1)}), s8[4194304]{0:T(1024)(128)(4,1)S(1)}, s32[]{:S(2)}) async-start(s8[7340032]{0:T(1024)(128)(4,1)} %bitcast.51), calls=%async_computation.2 | async-start | bytes 8388608
  24.0 86.8 %slice-start.3 = ((s8[7340032]{0:T(1024)(128)(4,1)}), s8[3145728]{0:T(1024)(128)(4,1)S(1)}, s32[]{:S(2)}) async-start(s8[7340032]{0:T(1024)(128)(4,1)} %bitcast.51), calls=%async_computation.3 | async-start | bytes 6291456
  114.2 6.2 %collective-permute-start.1 = (bf16[512,1792]{1,0:T(8,128)(2,1)}, bf16[512,1792]{1,0:T(8,128)(2,1)}, u32[]{:S(2)}, u32[]{:S(2)}) collective-permute-start(bf16[512,1792]{1,0:T(8,128)(2,1)} %fusion.9), channel_id=1, source_target_pairs={{0,1},{1,0},{2,3},{3,2},{4,5},{5,4},{6,7},{7,6},{8,9},{9,8},{10,11... | collective-permute-start | bytes 5505032 | tf_op jit(solution)/shard_map/ppermute | solution.py:254
  116.6 9.8 %copy-start.2 = (f32[1792]{0:T(1024)S(1)}, f32[1792]{0:T(1024)}, u32[]{:S(2)}) copy-start(f32[1792]{0:T(1024)} %param.13) | copy-start | bytes 21508
  125.1 1.2 collective-permute-start.2
where the time goes:
time: 128 us
  Pallas kernels  86.5 us (68%)
  matrix products  16.1 us (13%)
  other arithmetic  13.4 us (10%)
  waiting for transfers between devices  8.31 us (6%)
  starting transfers between devices  3.51 us (3%)
    pallas_call x1, Pallas kernels, attention(): pl.pallas_call(functools.partial(attention_kernel, blocks, rows), out_sha...  86.5 us
    ppermute x3, waiting for transfers between devices, swap_heads(): return lax.ppermute(shard, 'head', [(0, 1), (1, 0)])  8.31 us
    dot_general x3, matrix products, local(): jnp.dot(normed, weight, preferred_element_type=jnp.float32)  8.05 us
    dot_general x1, matrix products, local(): kept = jnp.dot(attended, mine, preferred_element_type=jnp.float32)  4.78 us
    reduce_sum x1, other arithmetic, local(): jnp.sum(widened * widened, axis=-1, keepdims=True) / widened.shape[-1]  4.53 us
    convert_element_type x1, other arithmetic, local(): normed = (widened * scale * pre_gain).astype(jnp.bfloat16)  3.81 us
    ppermute x3, starting transfers between devices, swap_heads(): return lax.ppermute(shard, 'head', [(0, 1), (1, 0)])  3.51 us
    dot_general x1, matrix products, local(): jnp.dot(attended, theirs, preferred_element_type=jnp.float32)  3.3 us
  transfers between devices with their start and end apart: 3, of which 3 were waited for; matrix products, arithmetic and copies ran while one was open for 0% of the time, Pallas kernels for 0%

commit v1 on v0

v1 whole, which is shorter than its diff:
```python
import functools
import math

import jax
import jax.numpy as jnp
from jax import lax
from jax.experimental import pallas as pl
from jax.experimental.pallas import tpu as pltpu
from jax.sharding import PartitionSpec as P

HD = 256
WINDOW = 4096

softcap_limit = 50.0
rope_base = 10000.0
norm_epsilon = 1e-06

ROW_TILE = 256

PIECES = 2
X_KV, X_Q, X_OUT, Z_NEAR, Z_FAR, Y_NEAR, Y_FAR, MESSAGES = 0, 2, 3, 5, 9, 13, 17, 21


def attention_kernel(
    blocks, rows, normed_ref, weight_ref, cosine_ref, sine_ref, kv_ref, out_ref,
    held, queries, asked, total, mass, leaving, landed, send_sems, recv_sems,
):
    group = 2 * 2
    me = lax.axis_index("seq")
    x = me % 2
    y = (me // 2) % 2
    x_mate = me + 1 - 2 * x
    y_mate = me + 2 - 4 * y
    z_next = me + group
    has_next = z_next < blocks
    has_prev = me >= group
    has_far = me >= 2 * group
    first_row = y == 0
    second_row = y == 1

    def copy(message, src, dst, device):
        return pltpu.make_async_remote_copy(
            src_ref=src,
            dst_ref=dst,
            send_sem=send_sems.at[message],
            recv_sem=recv_sems.at[message],
            device_id={"seq": device},
            device_id_type=pl.DeviceIdType.MESH,
        )

    barrier = pltpu.get_barrier_semaphore()

    def greet(device):
        pl.semaphore_signal(
            barrier, inc=1, device_id={"seq": device}, device_id_type=pl.DeviceIdType.MESH
        )

    greet(x_mate)
    greet(y_mate)
    pl.when(has_next)(lambda: greet(z_next))
    pl.when(has_prev)(lambda: greet(me - group))
    pl.semaphore_wait(barrier, 2 + has_next.astype(jnp.int32) + has_prev.astype(jnp.int32))

    pieces = [(r, h) for r in range(2) for h in range(PIECES)]
    near = lambda r, h: kv_ref.at[x, h] if r == 0 else held.at[0, 1, h]

    def copies(base, source, slot, device):
        return {
            (r, h): copy(base + PIECES * r + h, source(r, h), held.at[slot, r, h], device)
            for r, h in pieces
        }

    arrived = lambda slot: lambda r, h: held.at[slot, r, h]
    send_kv = [
        copy(X_KV + h, kv_ref.at[1 - x, h], held.at[0, 1, h], x_mate) for h in range(PIECES)
    ]
    send_q = copy(X_Q, asked, queries.at[1], x_mate)
    z_near = copies(Z_NEAR, near, 2, z_next)
    z_far = copies(Z_FAR, arrived(2), 4, z_next)
    y_up_near = copies(Y_NEAR, near, 1, y_mate)
    y_up_far = copies(Y_FAR, arrived(2), 3, y_mate)
    y_down_near = copies(Y_NEAR, arrived(2), 1, y_mate)
    y_down_far = copies(Y_FAR, arrived(4), 3, y_mate)

    for h in range(PIECES):
        send_kv[h].start()
        pl.when(has_next)(lambda: z_near[0, h].start())
        pl.when(first_row)(lambda: y_up_near[0, h].start())

    tiles_per_side = 2 * rows // ROW_TILE
    tiles_per_head = rows // ROW_TILE

    def ask(whose, store):
        def tile(t, carry):
            head = t // tiles_per_head
            start = pl.multiple_of((t % tiles_per_head) * ROW_TILE, ROW_TILE)
            at = pl.multiple_of((2 * whose + head) * HD, HD)
            value = jnp.dot(
                normed_ref[pl.ds(start, ROW_TILE), :],
                weight_ref[:, pl.ds(at, HD)],
                preferred_element_type=jnp.float32,
            )
            store(
                head,
                pl.ds(start, ROW_TILE),
                rotated(
                    value,
                    cosine_ref[pl.ds(start, ROW_TILE), :],
                    sine_ref[pl.ds(start, ROW_TILE), :],
                ),
            )
            return carry

        lax.fori_loop(0, tiles_per_side, tile, 0)

    def store_asked(head, where, value):
        asked[head, where, :] = value

    def store_own(head, where, value):
        queries[0, head, where, :] = value

    ask(1 - x, store_asked)

    def pass_mate(h):
        send_kv[h].wait_recv()
        pl.when(has_next)(lambda: z_near[1, h].start())
        pl.when(first_row)(lambda: y_up_near[1, h].start())

    def pass_near(r, h):
        z_near[r, h].wait_recv()
        pl.when(has_next)(lambda: z_far[r, h].start())
        pl.when(first_row)(lambda: y_up_far[r, h].start())
        pl.when(second_row)(lambda: y_down_near[r, h].start())

    def pass_far(r, h):
        z_far[r, h].wait_recv()
        pl.when(second_row)(lambda: y_down_far[r, h].start())

    pass_mate(0)
    pl.when(has_prev)(lambda: pass_near(0, 0))
    send_q.start()
    ask(x, store_own)
    total[...] = jnp.zeros_like(total)
    mass[...] = jnp.zeros_like(mass)
    pass_mate(1)
    pl.when(has_prev)(lambda: pass_near(0, 1))

    inner = 1.0 / (math.sqrt(HD) * softcap_limit)
    outer = softcap_limit / math.log(2.0)

    def attend(block, first, last, distances):
        keys_here = rows // PIECES

        def tile(t, carry):
            side = t // tiles_per_side
            within = t % tiles_per_side
            head = within // tiles_per_head
            start = pl.multiple_of((within % tiles_per_head) * ROW_TILE, ROW_TILE)
            q = queries[side, head, pl.ds(start, ROW_TILE), :]
            part = None
            added = None
            for h in range(PIECES):
                scores = lax.dot_general(
                    q, block[h, 0], (((1,), (1,)), ((), ())), preferred_element_type=jnp.float32
                )
                weights = jnp.exp2(outer * jnp.tanh(scores * inner))
                if distances is not None:
                    distance = jnp.where(side == 0, distances[0], distances[1])
                    offset = (
                        distance * rows
                        + start
                        - h * keys_here
                        + lax.broadcasted_iota(jnp.int32, weights.shape, 0)
                        - lax.broadcasted_iota(jnp.int32, weights.shape, 1)
                    )
                    weights = jnp.where((offset >= 0) & (offset < WINDOW), weights, 0.0)
                for k in range(keys_here // 128):
                    lanes = weights[:, k * 128 : (k + 1) * 128]
                    part = lanes if part is None else part + lanes
                product = jnp.dot(
                    weights.astype(jnp.bfloat16), block[h, 1], preferred_element_type=jnp.float32
                )
                added = product if added is None else added + product
            mass[side, head, pl.ds(start, ROW_TILE), :] += part
            total[side, head, pl.ds(start, ROW_TILE), :] += added
            return carry

        lax.fori_loop(first, last, tile, 0)

    both = 2 * tiles_per_side
    reach = WINDOW // rows

    def ahead(d, r, side):
        if side == r:
            return jnp.int32(2 * d)
        return 2 * d + (2 * x - 1 if side == 0 else 1 - 2 * x)

    def edge(d, r):
        return (ahead(d, r, 0), ahead(d, r, 1))

    def bounds(d, r):
        low, high = edge(d, r)
        fits = lambda e: (e >= 0) & (e <= reach)
        first = jnp.where(fits(low), 0, tiles_per_side)
        last = jnp.where(fits(high), both, tiles_per_side)
        return first, last

    def whole(slot, r):
        attend(held.at[slot, r], 0, both, None)

    def arrive_near(r):
        for h in range(PIECES):
            y_up_near[r, h].wait_recv()
        whole(1, r)

    def arrive_far(r):
        for h in range(PIECES):
            y_up_far[r, h].wait_recv()
        whole(3, r)

    def farthest(r):
        first, last = bounds(4, r)
        attend(held.at[4, r], first, last, edge(4, r))

    attend(kv_ref.at[x], 0, tiles_per_side, edge(0, 0))
    pl.when(has_prev)(lambda: pass_near(1, 0))
    send_q.wait_recv()
    pl.when(has_prev)(lambda: pass_near(1, 1))
    attend(kv_ref.at[x], tiles_per_side, bounds(0, 0)[1], edge(0, 0))
    first, last = bounds(0, 1)
    attend(held.at[0, 1], first, last, edge(0, 1))
    pl.when(has_far)(lambda: pass_far(0, 0))
    pl.when(has_prev)(lambda: whole(2, 0))
    pl.when(has_far)(lambda: pass_far(0, 1))
    pl.when(has_prev)(lambda: whole(2, 1))
    pl.when(me >= 2)(lambda: arrive_near(0))
    pl.when(has_far)(lambda: pass_far(1, 0))
    pl.when(has_far)(lambda: farthest(0))
    pl.when(has_far)(lambda: pass_far(1, 1))
    pl.when(me >= 2)(lambda: arrive_near(1))
    pl.when(has_far)(lambda: farthest(1))
    pl.when(me >= 6)(lambda: arrive_far(0))
    pl.when(me >= 6)(lambda: arrive_far(1))

    def finished(side, head):
        weight = jnp.sum(mass[side, head], axis=-1, keepdims=True)
        return (total[side, head] / weight).astype(jnp.bfloat16)

    send_out = [copy(X_OUT + head, leaving.at[head], landed.at[head], x_mate) for head in range(2)]
    leaving[0] = finished(1, 0)
    leaving[1] = finished(1, 1)
    send_out[0].start()
    for head in range(2):
        at = pl.multiple_of((2 * x + head) * HD, HD)
        out_ref[:, pl.ds(at, HD)] = finished(0, head)
        if head == 0:
            send_out[1].start()
    for head in range(2):
        send_out[head].wait_recv()
        at = pl.multiple_of((2 * (1 - x) + head) * HD, HD)
        out_ref[:, pl.ds(at, HD)] = landed[head]

    send_q.wait_send()
    for h in range(PIECES):
        send_kv[h].wait_send()
        send_out[h].wait_send()
    for r, h in pieces:
        pl.when(has_next)(lambda: z_near[r, h].wait_send())
        pl.when(has_next & has_prev)(lambda: z_far[r, h].wait_send())
        pl.when(first_row)(lambda: y_up_near[r, h].wait_send())
        pl.when(first_row & has_prev)(lambda: y_up_far[r, h].wait_send())
        pl.when(second_row & has_prev)(lambda: y_down_near[r, h].wait_send())
        pl.when(second_row & has_far)(lambda: y_down_far[r, h].wait_send())


def attention(normed, weight, cosine, sine, kv, blocks):
    rows = normed.shape[0]
    half = (2, rows, HD)
    vmem = pl.BlockSpec(memory_space=pltpu.VMEM)
    return pl.pallas_call(
        functools.partial(attention_kernel, blocks, rows),
        out_shape=jax.ShapeDtypeStruct((rows, 4 * HD), jnp.bfloat16),
        in_specs=[vmem] * 5,
        out_specs=vmem,
        scratch_shapes=[
            pltpu.VMEM((5, 2) + kv.shape[1:], jnp.bfloat16),
            pltpu.VMEM((2,) + half, jnp.bfloat16),
            pltpu.VMEM(half, jnp.bfloat16),
            pltpu.VMEM((2,) + half, jnp.float32),
            pltpu.VMEM((2, 2, rows, 128), jnp.float32),
            pltpu.VMEM(half, jnp.bfloat16),
            pltpu.VMEM(half, jnp.bfloat16),
            pltpu.SemaphoreType.DMA((MESSAGES,)),
            pltpu.SemaphoreType.DMA((MESSAGES,)),
        ],
        compiler_params=pltpu.CompilerParams(
            collective_id=0, has_side_effects=True, vmem_limit_bytes=48 * 1024 * 1024
        ),
    )(normed, weight, cosine, sine, kv)


def norm_kernel(own_ref, other_ref, gain_ref, out_ref):
    side = lax.axis_index("head")
    width = own_ref.shape[1]
    own = own_ref[...].astype(jnp.float32)
    other = other_ref[...].astype(jnp.float32)
    squares = jnp.sum(own * own, axis=-1, keepdims=True)
    squares = squares + jnp.sum(other * other, axis=-1, keepdims=True)
    scale = lax.rsqrt(squares / (2 * width) + norm_epsilon)
    for values, place in ((own, side), (other, 1 - side)):
        at = pl.ds(pl.multiple_of(place * width, width), width)
        out_ref[:, at] = (values * scale * gain_ref[:, at]).astype(jnp.bfloat16)


def norm(own, other, gain):
    rows, width = own.shape
    step = rows // 8
    return pl.pallas_call(
        norm_kernel,
        grid=(rows // step,),
        out_shape=jax.ShapeDtypeStruct((rows, 2 * width), jnp.bfloat16),
        in_specs=[
            pl.BlockSpec((step, width), lambda i: (i, 0)),
            pl.BlockSpec((step, width), lambda i: (i, 0)),
            pl.BlockSpec((1, 2 * width), lambda i: (0, 0)),
        ],
        out_specs=pl.BlockSpec((step, 2 * width), lambda i: (i, 0)),
    )(own, other, gain[None, :])


def swap_heads(shard):
    return lax.ppermute(shard, "head", [(0, 1), (1, 0)])


def rope_tables(positions):
    midpoint = HD // 2
    frequency = jnp.exp(
        -jnp.log(rope_base) * (2.0 * jnp.arange(midpoint, dtype=jnp.float32) / HD)
    )
    angles = positions.astype(jnp.float32)[:, None] * frequency[None, :]
    return jnp.cos(angles), jnp.sin(angles)


def rotated(head, cosine, sine):
    midpoint = HD // 2
    leading, trailing = head[:, :midpoint], head[:, midpoint:]
    return jnp.concatenate(
        [leading * cosine - trailing * sine, trailing * cosine + leading * sine], axis=-1
    ).astype(jnp.bfloat16)


def local(blocks, tokens, pre_gain, query_weight, key_weight, value_weight, out_weight, post_gain):
    rows, width = tokens.shape
    side = lax.axis_index("head")
    other = swap_heads(tokens)
    normed = norm(tokens, other, pre_gain)
    positions = lax.axis_index("seq") * rows + jnp.arange(rows, dtype=jnp.int32)
    cosine, sine = rope_tables(positions)
    project = lambda weight: jnp.dot(normed, weight, preferred_element_type=jnp.float32)
    k_all, v_all = project(key_weight), project(value_weight)
    head_of = lambda a, h: a[:, h * HD : (h + 1) * HD]
    in_pieces = lambda a: a.reshape(PIECES, rows // PIECES, HD)
    kv = jnp.stack(
        [
            jnp.stack(
                [
                    in_pieces(rotated(head_of(k_all, k), cosine, sine)),
                    in_pieces(head_of(v_all, k).astype(jnp.bfloat16)),
                ],
                axis=1,
            )
            for k in range(2)
        ]
    )
    attended = attention(normed, query_weight, cosine, sine, kv, blocks)
    mine = lax.dynamic_slice_in_dim(out_weight, side * width, width, 1)
    theirs = lax.dynamic_slice_in_dim(out_weight, (1 - side) * width, width, 1)
    given = jnp.dot(attended, theirs, preferred_element_type=jnp.float32).astype(jnp.bfloat16)
    arrived = swap_heads(given)
    kept = jnp.dot(attended, mine, preferred_element_type=jnp.float32)
    share = kept + arrived.astype(jnp.float32)
    squares = jnp.sum(share * share, axis=1, keepdims=True)
    squares = squares + swap_heads(squares)
    inverse_rms = lax.rsqrt(squares / (2 * width) + norm_epsilon)
    return (tokens.astype(jnp.float32) + post_gain * share * inverse_rms).astype(jnp.bfloat16)


def solution(mesh):
    placed = (
        P("seq", "head"),
        P(),
        P(None, "head"),
        P(None, "head"),
        P(None, "head"),
        P("head", None),
        P("head"),
    )
    return jax.shard_map(
        functools.partial(local, mesh.shape["seq"]),
        mesh=mesh,
        in_specs=placed,
        out_specs=P("seq", "head"),
        check_vma=False,
    )
```

time: 128 us -> 122 us (0.953)
  other arithmetic: 13.4 us -> 3.39 us
  Pallas kernels: 86.5 us -> 90 us
  local copies, waits for them, and re-layouts: 0.3 us -> 2.61 us
  waiting for transfers between devices: 8.31 us -> 6.72 us
    pallas_call x0 -> x1, Pallas kernels: none -> 7.17 us  [norm(): pl.pallas_call(norm_kernel, grid=(rows // step,), out_shape=jax.ShapeDtyp...]
    reduce_sum x1 -> x0, other arithmetic: 4.53 us -> none  [local(): jnp.sum(widened * widened, axis=-1, keepdims=True) / widened.shape[-1]]
    convert_element_type x1 -> x0, other arithmetic: 3.81 us -> none  [local(): normed = (widened * scale * pre_gain).astype(jnp.bfloat16)]
    pallas_call x1, Pallas kernels: 86.5 us -> 82.8 us  [attention(): pl.pallas_call(functools.partial(attention_kernel, blocks, rows), out_sha...]
    concatenate x2 -> x0, other arithmetic: 2.67 us -> none  [rotated(): jnp.concatenate([leading * cosine - trailing * sine, trailing * cosine +...]
    ppermute x3, waiting for transfers between devices: 8.31 us -> 6.72 us  [swap_heads(): return lax.ppermute(shard, 'head', [(0, 1), (1, 0)])]
    broadcast_in_dim x0 -> x1, local copies, waits for them, and re-layouts: none -> 1.32 us  [norm(): gain[None, :]]
    dot_general x3 -> x2, matrix products: 8.05 us -> 7.39 us  [local(): jnp.dot(normed, weight, preferred_element_type=jnp.float32)]
  transfers between devices with their start and end apart: 3 -> 3, of which waited for: 3 -> 3; matrix products, arithmetic and copies ran while one was open for 0% -> 1% of each run, Pallas kernels for 0% -> 0%
where the time goes in v1:
time: 122 us
  Pallas kernels  90 us (74%)
  matrix products  14.9 us (12%)
  waiting for transfers between devices  6.72 us (6%)
  starting transfers between devices  3.79 us (3%)
  other arithmetic  3.39 us (3%)
  local copies, waits for them, and re-layouts  2.61 us (2%)
    pallas_call x1, Pallas kernels, attention(): pl.pallas_call(functools.partial(attention_kernel, blocks, rows), out_sha...  82.8 us
    dot_general x2, matrix products, local(): jnp.dot(normed, weight, preferred_element_type=jnp.float32)  7.39 us
    pallas_call x1, Pallas kernels, norm(): pl.pallas_call(norm_kernel, grid=(rows // step,), out_shape=jax.ShapeDtyp...  7.17 us
    ppermute x3, waiting for transfers between devices, swap_heads(): return lax.ppermute(shard, 'head', [(0, 1), (1, 0)])  6.72 us
    dot_general x1, matrix products, local(): kept = jnp.dot(attended, mine, preferred_element_type=jnp.float32)  4.2 us
    ppermute x3, starting transfers between devices, swap_heads(): return lax.ppermute(shard, 'head', [(0, 1), (1, 0)])  3.79 us
    dot_general x1, matrix products, local(): jnp.dot(attended, theirs, preferred_element_type=jnp.float32)  3.3 us
  transfers between devices with their start and end apart: 3, of which 3 were waited for; matrix products, arithmetic and copies ran while one was open for 1% of the time, Pallas kernels for 0%

profile of v1, /device:TPU:17, one launch (start us, length us, event | category | flops | bytes accessed | tf_op | source)
XLA Modules:
  0.0 121.5 jit_solution(13759512580857175154)
XLA Ops:
  0.0 0.7 collective-permute-start
  0.7 1.3 %broadcast_in_dim.4.gain_ref = f32[1,3584]{1,0:T(1,128)} reshape(f32[3584]{0:T(1024)} %param.8) | data formatting | bytes 28672 | tf_op jit(solution)/shard_map/broadcast_in_dim | solution.py:328
  2.0 2.3 %collective-permute-done.other_ref = bf16[512,1792]{1,0:T(8,128)(2,1)S(1)} collective-permute-done((bf16[512,1792]{1,0:T(8,128)(2,1)}, bf16[512,1792]{1,0:T(8,128)(2,1)S(1)}, u32[]{:S(2)}, u32[]{:S(2)}) %collective-permute-start) | collective-permute-done | bytes 1835040 | tf_op jit(solution)/shard_map/ppermute | solution.py:332
  4.3 0.0 copy-start.2
  4.3 1.2 %copy-done.2 = bf16[512,1792]{1,0:T(8,128)(2,1)} copy-done((bf16[512,1792]{1,0:T(8,128)(2,1)}, bf16[512,1792]{1,0:T(8,128)(2,1)S(1)}, u32[]{:S(2)}) %copy-start.2) | copy-done | bytes 1835032
  5.5 7.2 %shard_map.73.normed_ref = bf16[512,3584]{1,0:T(8,128)(2,1)} custom-call(bf16[512,1792]{1,0:T(8,128)(2,1)} %own_ref.1, bf16[512,1792]{1,0:T(8,128)(2,1)} %copy-done.2, f32[1,3584]{1,0:T(1,128)} %broadcast_in_dim.4.gain_ref), custom_call_target="tpu_custom_call" | custom-call | tf_op jit(solution)/shard_map/pallas_call | solution.py:318
  12.7 0.0 copy-start
  12.7 0.0 copy-start.4
  12.7 5.3 %convolution_convert_fusion = bf16[512,512]{1,0:T(8,128)(2,1)S(1)} fusion(bf16[512,3584]{1,0:T(8,128)(2,1)} %shard_map.73.normed_ref, bf16[3584,512]{1,0:T(8,128)(2,1)} %param.11), kind=kOutput, calls=%fused_computation.8 | convolution fusion | flops 1879310336 | bytes 7864320 | tf_op jit(solution)/shard_map/dot_general | solution.py:359
  18.1 0.0 copy-done
  18.1 0.0 copy-done.4
  18.1 2.1 %fusion.28 = f32[512,512]{1,0:T(8,128)S(1)} fusion(bf16[512,3584]{1,0:T(8,128)(2,1)S(1)} %copy-done, bf16[3584,512]{1,0:T(8,128)(2,1)S(1)} %copy-done.4), kind=kOutput, calls=%fused_computation.36 | convolution fusion | flops 1879048192 | bytes 8388608 | tf_op jit(solution)/shard_map/dot_general | solution.py:359
  20.2 1.3 %fusion.18 = (bf16[512,128]{1,0:T(8,128)(2,1)S(1)}, bf16[512,128]{1,0:T(8,128)(2,1)S(1)}, bf16[512,128]{1,0:T(8,128)(2,1)S(1)}, bf16[512,128]{1,0:T(8,128)(2,1)S...) fusion(f32[512,512]{1,0:T(8,128)S(1)} %fusion.28, f32[128]{0:T(128)S(1)} %multiply_exponential_fusion, ...), kind=kLoop, calls=%fused_computation.23 | loop fusion | flops 1114112 | bytes 2099712 | tf_op jit(solution)/shard_map/convert.9
  21.4 0.1 maximum_bitcast_fusion
  21.5 0.0 slice-start
  21.6 0.1 pad_maximum_fusion.kv_ref
  21.7 0.0 slice-start.1
  21.7 82.8 %shard_map.74 = bf16[512,1024]{1,0:T(8,128)(2,1)S(1)} custom-call(bf16[512,3584]{1,0:T(8,128)(2,1)} %shard_map.73.normed_ref, bf16[3584,1024]{1,0:T(8,128)(2,1)} %weight_ref.1, f32[512,128]{1,0:T(8,128)S(1)} %get-tuple-element.12.cosine_ref, f32[512,128]{1,0:T(8,128)S(1)} %get-tuple-element.11.sine_ref, bf16[2,2,2,256,256]{4,3,2,1,0:T(8,128)(2,1)S(1)} %pad_maximum_fusion.kv_ref), custom_call_target="tpu_custom_call" | custom-call | tf_op jit(solution)/shard_map/pallas_call | solution.py:280
  104.5 0.0 slice-done
  104.5 0.0 slice-done.1
  104.5 3.3 %fusion.6 = bf16[512,1792]{1,0:T(8,128)(2,1)} fusion(bf16[512,1024]{1,0:T(8,128)(2,1)S(1)} %shard_map.74, bf16[1024,3584]{1,0:T(8,128)(2,1)S(1)} %bitcast.28, s32[]{:T(128)S(6)} %select_n.7), kind=kOutput, calls=%fused_computation.7 | convolution fusion | flops 1879965696 | bytes 6553604 | tf_op jit(solution)/shard_map/dot_general | solution.py:378
  107.8 2.7 %collective-permute-start.1 = (bf16[512,1792]{1,0:T(8,128)(2,1)}, bf16[512,1792]{1,0:T(8,128)(2,1)S(1)}, u32[]{:S(2)}, u32[]{:S(2)}) collective-permute-start(bf16[512,1792]{1,0:T(8,128)(2,1)} %fusion.6), channel_id=1, source_target_pairs={{0,1},{1,0},{2,3},{3,2},{4,5},{5,4},{6,7},{7,6},{8,9},{9,8},{10,11... | collective-permute-start | bytes 5505032 | tf_op jit(solution)/shard_map/ppermute | solution.py:332
  110.5 0.0 copy-start.1
  110.5 0.0 copy-start.3
  110.5 3.6 %collective-permute-done.1 = bf16[512,1792]{1,0:T(8,128)(2,1)S(1)} collective-permute-done((bf16[512,1792]{1,0:T(8,128)(2,1)}, bf16[512,1792]{1,0:T(8,128)(2,1)S(1)}, u32[]{:S(2)}, u32[]{:S(2)}) %collective-permute-start.1) | collective-permute-done | bytes 1835040 | tf_op jit(solution)/shard_map/ppermute | solution.py:332
  114.1 4.2 %multiply_reduce_fusion = (f32[512]{0:T(512)S(1)}, f32[512,1792]{1,0:T(8,128)S(1)}) fusion(bf16[512,1792]{1,0:T(8,128)(2,1)S(1)} %collective-permute-done.1, bf16[512,1024]{1,0:T(8,128)(2,1)S(1)} %shard_map.74, bf16[1024,3584]{1,0:T(8,128)(2,1)} %param.12, s32[]{:T(128)S(6)} %select_n.6), kind=kOutput, calls=%fused_computation.1 | convolution fusion | flops 1882717696 | bytes 10225668 | tf_op jit(solution)/shard_map/dot_general | solution.py:380
  118.3 0.4 collective-permute-start.2
  118.8 0.8 collective-permute-done.2
  119.6 0.0 copy-done.1
  119.6 0.0 copy-done.3
  119.6 1.9 %add_convert_fusion = bf16[512,1792]{1,0:T(8,128)(2,1)} fusion(f32[512,1792]{1,0:T(8,128)S(1)} %get-tuple-element.14, bf16[512,1792]{1,0:T(8,128)(2,1)S(1)} %copy-done.1, f32[512]{0:T(512)S(1)} %bitcast.24, f32[1792]{0:T(1024)S(1)} %copy-done.3), kind=kLoop, calls=%fused_computation | loop fusion | flops 4587520 | bytes 7349248 | tf_op jit(solution)/shard_map/convert_element_type | solution.py:385
  (5 shorter events, 0.1 us)
Async XLA Ops:
  0.0 4.3 %collective-permute-start = (bf16[512,1792]{1,0:T(8,128)(2,1)}, bf16[512,1792]{1,0:T(8,128)(2,1)S(1)}, u32[]{:S(2)}, u32[]{:S(2)}) collective-permute-start(bf16[512,1792]{1,0:T(8,128)(2,1)} %own_ref.1), channel_id=1, source_target_pairs={{0,1},{1,0},{2,3},{3,2},{4,5},{5,4},{6,7},{7,6},{8,9},{9,8},{10,11... | collective-permute-start | bytes 5505032 | tf_op jit(solution)/shard_map/ppermute | solution.py:332
  4.3 1.2 %copy-start.2 = (bf16[512,1792]{1,0:T(8,128)(2,1)}, bf16[512,1792]{1,0:T(8,128)(2,1)S(1)}, u32[]{:S(2)}) copy-start(bf16[512,1792]{1,0:T(8,128)(2,1)S(1)} %collective-permute-done.other_ref) | copy-start | bytes 5505028
  12.7 5.4 %copy-start = (bf16[512,3584]{1,0:T(8,128)(2,1)S(1)}, bf16[512,3584]{1,0:T(8,128)(2,1)}, u32[]{:S(2)}) copy-start(bf16[512,3584]{1,0:T(8,128)(2,1)} %shard_map.73.normed_ref) | copy-start | bytes 11010052
  12.7 5.4 %copy-start.4 = (bf16[3584,512]{1,0:T(8,128)(2,1)S(1)}, bf16[3584,512]{1,0:T(8,128)(2,1)}, u32[]{:S(2)}) copy-start(bf16[3584,512]{1,0:T(8,128)(2,1)} %param.10) | copy-start | bytes 11010052
  21.5 83.0 %slice-start = ((s8[7340032]{0:T(1024)(128)(4,1)}), s8[4194304]{0:T(1024)(128)(4,1)S(1)}, s32[]{:S(2)}) async-start(s8[7340032]{0:T(1024)(128)(4,1)} %bitcast.27), calls=%async_computation | async-start | bytes 8388608
  21.7 82.9 %slice-start.1 = ((s8[7340032]{0:T(1024)(128)(4,1)}), s8[3145728]{0:T(1024)(128)(4,1)S(1)}, s32[]{:S(2)}) async-start(s8[7340032]{0:T(1024)(128)(4,1)} %bitcast.27), calls=%async_computation.1 | async-start | bytes 6291456
  107.8 6.3 %collective-permute-start.1 = (bf16[512,1792]{1,0:T(8,128)(2,1)}, bf16[512,1792]{1,0:T(8,128)(2,1)S(1)}, u32[]{:S(2)}, u32[]{:S(2)}) collective-permute-start(bf16[512,1792]{1,0:T(8,128)(2,1)} %fusion.6), channel_id=1, source_target_pairs={{0,1},{1,0},{2,3},{3,2},{4,5},{5,4},{6,7},{7,6},{8,9},{9,8},{10,11... | collective-permute-start | bytes 5505032 | tf_op jit(solution)/shard_map/ppermute | solution.py:332
  110.5 9.1 %copy-start.1 = (bf16[512,1792]{1,0:T(8,128)(2,1)S(1)}, bf16[512,1792]{1,0:T(8,128)(2,1)}, u32[]{:S(2)}) copy-start(bf16[512,1792]{1,0:T(8,128)(2,1)} %own_ref.1) | copy-start | bytes 5505028
  110.5 9.1 %copy-start.3 = (f32[1792]{0:T(1024)S(1)}, f32[1792]{0:T(1024)}, u32[]{:S(2)}) copy-start(f32[1792]{0:T(1024)} %param.13) | copy-start | bytes 21508
  118.3 1.3 %collective-permute-start.2 = (f32[512,1]{0,1:T(1,128)S(1)}, f32[512,1]{0,1:T(1,128)S(1)}, u32[]{:S(2)}, u32[]{:S(2)}) collective-permute-start(f32[512,1]{0,1:T(1,128)S(1)} %bitcast.25), channel_id=1, source_target_pairs={{0,1},{1,0},{2,3},{3,2},{4,5},{5,4},{6,7},{7,6},{8,9},{9,8},{10,11... | collective-permute-start | bytes 6152 | tf_op jit(solution)/shard_map/ppermute | solution.py:332

commit v2 on v1

--- a/solution.py
+++ b/solution.py
@@ -15,7 +15,7 @@
 rope_base = 10000.0
 norm_epsilon = 1e-06
 
-ROW_TILE = 256
+ROW_TILE = 512
 
 PIECES = 2
 X_KV, X_Q, X_OUT, Z_NEAR, Z_FAR, Y_NEAR, Y_FAR, MESSAGES = 0, 2, 3, 5, 9, 13, 17, 21
@@ -302,19 +302,27 @@
 def norm_kernel(own_ref, other_ref, gain_ref, out_ref):
     side = lax.axis_index("head")
     width = own_ref.shape[1]
-    own = own_ref[...].astype(jnp.float32)
-    other = other_ref[...].astype(jnp.float32)
-    squares = jnp.sum(own * own, axis=-1, keepdims=True)
-    squares = squares + jnp.sum(other * other, axis=-1, keepdims=True)
-    scale = lax.rsqrt(squares / (2 * width) + norm_epsilon)
-    for values, place in ((own, side), (other, 1 - side)):
-        at = pl.ds(pl.multiple_of(place * width, width), width)
-        out_ref[:, at] = (values * scale * gain_ref[:, at]).astype(jnp.bfloat16)
+    lines = 16
+
+    def chunk(i, carry):
+        at_rows = pl.ds(pl.multiple_of(i * lines, lines), lines)
+        squares = jnp.zeros((lines, 1), jnp.float32)
+        for ref in (own_ref, other_ref):
+            values = ref[at_rows, :].astype(jnp.float32)
+            squares = squares + jnp.sum(values * values, axis=-1, keepdims=True)
+        scale = lax.rsqrt(squares / (2 * width) + norm_epsilon)
+        for ref, place in ((own_ref, side), (other_ref, 1 - side)):
+            at = pl.ds(pl.multiple_of(place * width, width), width)
+            values = ref[at_rows, :].astype(jnp.float32)
+            out_ref[at_rows, at] = (values * scale * gain_ref[:, at]).astype(jnp.bfloat16)
+        return carry
+
+    lax.fori_loop(0, own_ref.shape[0] // lines, chunk, 0, unroll=2)
 
 
 def norm(own, other, gain):
     rows, width = own.shape
-    step = rows // 8
+    step = rows // 4
     return pl.pallas_call(
         norm_kernel,
         grid=(rows // step,),

time: 122 us -> 115 us (0.943)
  Pallas kernels: 90 us -> 82.9 us
    pallas_call x1, Pallas kernels: 82.8 us -> 77.2 us  [attention(): pl.pallas_call(functools.partial(attention_kernel, blocks, rows), out_sha...]
    pallas_call x1, Pallas kernels: 7.17 us -> 5.61 us  [norm(): pl.pallas_call(norm_kernel, grid=(rows // step,), out_shape=jax.ShapeDtyp...]
where the time goes in v2:
time: 115 us
  Pallas kernels  82.9 us (72%)
  matrix products  14.9 us (13%)
  waiting for transfers between devices  6.72 us (6%)
  starting transfers between devices  4.35 us (4%)
  other arithmetic  3.39 us (3%)
  local copies, waits for them, and re-layouts  2.61 us (2%)
    pallas_call x1, Pallas kernels, attention(): pl.pallas_call(functools.partial(attention_kernel, blocks, rows), out_sha...  77.2 us
    dot_general x2, matrix products, local(): jnp.dot(normed, weight, preferred_element_type=jnp.float32)  7.39 us
    ppermute x3, waiting for transfers between devices, swap_heads(): return lax.ppermute(shard, 'head', [(0, 1), (1, 0)])  6.72 us
    pallas_call x1, Pallas kernels, norm(): pl.pallas_call(norm_kernel, grid=(rows // step,), out_shape=jax.ShapeDtyp...  5.61 us
    ppermute x3, starting transfers between devices, swap_heads(): return lax.ppermute(shard, 'head', [(0, 1), (1, 0)])  4.35 us
    dot_general x1, matrix products, local(): kept = jnp.dot(attended, mine, preferred_element_type=jnp.float32)  4.2 us
    dot_general x1, matrix products, local(): jnp.dot(attended, theirs, preferred_element_type=jnp.float32)  3.3 us
  transfers between devices with their start and end apart: 3, of which 3 were waited for; matrix products, arithmetic and copies ran while one was open for 1% of the time, Pallas kernels for 0%

profile of v2, /device:TPU:17, one launch (start us, length us, event | category | flops | bytes accessed | tf_op | source)
XLA Modules:
  0.0 115.0 jit_solution(757382097911143496)
XLA Ops:
  0.0 0.7 collective-permute-start
  0.7 1.3 %broadcast_in_dim.4.gain_ref = f32[1,3584]{1,0:T(1,128)} reshape(f32[3584]{0:T(1024)} %param.8) | data formatting | bytes 28672 | tf_op jit(solution)/shard_map/broadcast_in_dim | solution.py:336
  2.0 2.3 %collective-permute-done.other_ref = bf16[512,1792]{1,0:T(8,128)(2,1)S(1)} collective-permute-done((bf16[512,1792]{1,0:T(8,128)(2,1)}, bf16[512,1792]{1,0:T(8,128)(2,1)S(1)}, u32[]{:S(2)}, u32[]{:S(2)}) %collective-permute-start) | collective-permute-done | bytes 1835040 | tf_op jit(solution)/shard_map/ppermute | solution.py:340
  4.3 0.0 copy-start.2
  4.3 1.2 %copy-done.2 = bf16[512,1792]{1,0:T(8,128)(2,1)} copy-done((bf16[512,1792]{1,0:T(8,128)(2,1)}, bf16[512,1792]{1,0:T(8,128)(2,1)S(1)}, u32[]{:S(2)}) %copy-start.2) | copy-done | bytes 1835032
  5.5 5.6 %shard_map.73.normed_ref = bf16[512,3584]{1,0:T(8,128)(2,1)} custom-call(bf16[512,1792]{1,0:T(8,128)(2,1)} %own_ref.1, bf16[512,1792]{1,0:T(8,128)(2,1)} %copy-done.2, f32[1,3584]{1,0:T(1,128)} %broadcast_in_dim.4.gain_ref), custom_call_target="tpu_custom_call" | custom-call | tf_op jit(solution)/shard_map/pallas_call | solution.py:326
  11.1 0.0 copy-start
  11.1 0.0 copy-start.4
  11.1 5.3 %convolution_convert_fusion = bf16[512,512]{1,0:T(8,128)(2,1)S(1)} fusion(bf16[512,3584]{1,0:T(8,128)(2,1)} %shard_map.73.normed_ref, bf16[3584,512]{1,0:T(8,128)(2,1)} %param.11), kind=kOutput, calls=%fused_computation.8 | convolution fusion | flops 1879310336 | bytes 7864320 | tf_op jit(solution)/shard_map/dot_general | solution.py:367
  16.5 0.0 copy-done
  16.5 0.0 copy-done.4
  16.6 2.1 %fusion.28 = f32[512,512]{1,0:T(8,128)S(1)} fusion(bf16[512,3584]{1,0:T(8,128)(2,1)S(1)} %copy-done, bf16[3584,512]{1,0:T(8,128)(2,1)S(1)} %copy-done.4), kind=kOutput, calls=%fused_computation.36 | convolution fusion | flops 1879048192 | bytes 8388608 | tf_op jit(solution)/shard_map/dot_general | solution.py:367
  18.6 1.3 %fusion.18 = (bf16[512,128]{1,0:T(8,128)(2,1)S(1)}, bf16[512,128]{1,0:T(8,128)(2,1)S(1)}, bf16[512,128]{1,0:T(8,128)(2,1)S(1)}, bf16[512,128]{1,0:T(8,128)(2,1)S...) fusion(f32[512,512]{1,0:T(8,128)S(1)} %fusion.28, f32[128]{0:T(128)S(1)} %multiply_exponential_fusion, ...), kind=kLoop, calls=%fused_computation.23 | loop fusion | flops 1114112 | bytes 2099712 | tf_op jit(solution)/shard_map/convert.9
  19.9 0.1 maximum_bitcast_fusion
  20.0 0.0 slice-start
  20.0 0.1 pad_maximum_fusion.kv_ref
  20.1 0.0 slice-start.1
  20.1 77.2 %shard_map.74 = bf16[512,1024]{1,0:T(8,128)(2,1)S(1)} custom-call(bf16[512,3584]{1,0:T(8,128)(2,1)} %shard_map.73.normed_ref, bf16[3584,1024]{1,0:T(8,128)(2,1)} %weight_ref.1, f32[512,128]{1,0:T(8,128)S(1)} %get-tuple-element.12.cosine_ref, f32[512,128]{1,0:T(8,128)S(1)} %get-tuple-element.11.sine_ref, bf16[2,2,2,256,256]{4,3,2,1,0:T(8,128)(2,1)S(1)} %pad_maximum_fusion.kv_ref), custom_call_target="tpu_custom_call" | custom-call | tf_op jit(solution)/shard_map/pallas_call | solution.py:280
  97.4 0.0 slice-done
  97.4 0.0 slice-done.1
  97.4 3.3 %fusion.6 = bf16[512,1792]{1,0:T(8,128)(2,1)} fusion(bf16[512,1024]{1,0:T(8,128)(2,1)S(1)} %shard_map.74, bf16[1024,3584]{1,0:T(8,128)(2,1)S(1)} %bitcast.28, s32[]{:T(128)S(6)} %select_n.7), kind=kOutput, calls=%fused_computation.7 | convolution fusion | flops 1879965696 | bytes 6553604 | tf_op jit(solution)/shard_map/dot_general | solution.py:386
  100.7 3.2 %collective-permute-start.1 = (bf16[512,1792]{1,0:T(8,128)(2,1)}, bf16[512,1792]{1,0:T(8,128)(2,1)S(1)}, u32[]{:S(2)}, u32[]{:S(2)}) collective-permute-start(bf16[512,1792]{1,0:T(8,128)(2,1)} %fusion.6), channel_id=1, source_target_pairs={{0,1},{1,0},{2,3},{3,2},{4,5},{5,4},{6,7},{7,6},{8,9},{9,8},{10,11... | collective-permute-start | bytes 5505032 | tf_op jit(solution)/shard_map/ppermute | solution.py:340
  103.9 0.0 copy-start.1
  103.9 0.0 copy-start.3
  103.9 3.6 %collective-permute-done.1 = bf16[512,1792]{1,0:T(8,128)(2,1)S(1)} collective-permute-done((bf16[512,1792]{1,0:T(8,128)(2,1)}, bf16[512,1792]{1,0:T(8,128)(2,1)S(1)}, u32[]{:S(2)}, u32[]{:S(2)}) %collective-permute-start.1) | collective-permute-done | bytes 1835040 | tf_op jit(solution)/shard_map/ppermute | solution.py:340
  107.6 4.2 %multiply_reduce_fusion = (f32[512]{0:T(512)S(1)}, f32[512,1792]{1,0:T(8,128)S(1)}) fusion(bf16[512,1792]{1,0:T(8,128)(2,1)S(1)} %collective-permute-done.1, bf16[512,1024]{1,0:T(8,128)(2,1)S(1)} %shard_map.74, bf16[1024,3584]{1,0:T(8,128)(2,1)} %param.12, s32[]{:T(128)S(6)} %select_n.6), kind=kOutput, calls=%fused_computation.1 | convolution fusion | flops 1882717696 | bytes 10225668 | tf_op jit(solution)/shard_map/dot_general | solution.py:388
  111.8 0.4 collective-permute-start.2
  112.2 0.8 collective-permute-done.2
  113.0 0.0 copy-done.1
  113.0 0.0 copy-done.3
  113.1 1.9 %add_convert_fusion = bf16[512,1792]{1,0:T(8,128)(2,1)} fusion(f32[512,1792]{1,0:T(8,128)S(1)} %get-tuple-element.14, bf16[512,1792]{1,0:T(8,128)(2,1)S(1)} %copy-done.1, f32[512]{0:T(512)S(1)} %bitcast.24, f32[1792]{0:T(1024)S(1)} %copy-done.3), kind=kLoop, calls=%fused_computation | loop fusion | flops 4587520 | bytes 7349248 | tf_op jit(solution)/shard_map/convert_element_type | solution.py:393
  (5 shorter events, 0.1 us)
Async XLA Ops:
  0.0 4.3 %collective-permute-start = (bf16[512,1792]{1,0:T(8,128)(2,1)}, bf16[512,1792]{1,0:T(8,128)(2,1)S(1)}, u32[]{:S(2)}, u32[]{:S(2)}) collective-permute-start(bf16[512,1792]{1,0:T(8,128)(2,1)} %own_ref.1), channel_id=1, source_target_pairs={{0,1},{1,0},{2,3},{3,2},{4,5},{5,4},{6,7},{7,6},{8,9},{9,8},{10,11... | collective-permute-start | bytes 5505032 | tf_op jit(solution)/shard_map/ppermute | solution.py:340
  4.3 1.2 %copy-start.2 = (bf16[512,1792]{1,0:T(8,128)(2,1)}, bf16[512,1792]{1,0:T(8,128)(2,1)S(1)}, u32[]{:S(2)}) copy-start(bf16[512,1792]{1,0:T(8,128)(2,1)S(1)} %collective-permute-done.other_ref) | copy-start | bytes 5505028
  11.1 5.4 %copy-start = (bf16[512,3584]{1,0:T(8,128)(2,1)S(1)}, bf16[512,3584]{1,0:T(8,128)(2,1)}, u32[]{:S(2)}) copy-start(bf16[512,3584]{1,0:T(8,128)(2,1)} %shard_map.73.normed_ref) | copy-start | bytes 11010052
  11.1 5.4 %copy-start.4 = (bf16[3584,512]{1,0:T(8,128)(2,1)S(1)}, bf16[3584,512]{1,0:T(8,128)(2,1)}, u32[]{:S(2)}) copy-start(bf16[3584,512]{1,0:T(8,128)(2,1)} %param.10) | copy-start | bytes 11010052
  20.0 77.4 %slice-start = ((s8[7340032]{0:T(1024)(128)(4,1)}), s8[4194304]{0:T(1024)(128)(4,1)S(1)}, s32[]{:S(2)}) async-start(s8[7340032]{0:T(1024)(128)(4,1)} %bitcast.27), calls=%async_computation | async-start | bytes 8388608
  20.1 77.3 %slice-start.1 = ((s8[7340032]{0:T(1024)(128)(4,1)}), s8[3145728]{0:T(1024)(128)(4,1)S(1)}, s32[]{:S(2)}) async-start(s8[7340032]{0:T(1024)(128)(4,1)} %bitcast.27), calls=%async_computation.1 | async-start | bytes 6291456
  100.7 6.9 %collective-permute-start.1 = (bf16[512,1792]{1,0:T(8,128)(2,1)}, bf16[512,1792]{1,0:T(8,128)(2,1)S(1)}, u32[]{:S(2)}, u32[]{:S(2)}) collective-permute-start(bf16[512,1792]{1,0:T(8,128)(2,1)} %fusion.6), channel_id=1, source_target_pairs={{0,1},{1,0},{2,3},{3,2},{4,5},{5,4},{6,7},{7,6},{8,9},{9,8},{10,11... | collective-permute-start | bytes 5505032 | tf_op jit(solution)/shard_map/ppermute | solution.py:340
  103.9 9.1 %copy-start.1 = (bf16[512,1792]{1,0:T(8,128)(2,1)S(1)}, bf16[512,1792]{1,0:T(8,128)(2,1)}, u32[]{:S(2)}) copy-start(bf16[512,1792]{1,0:T(8,128)(2,1)} %own_ref.1) | copy-start | bytes 5505028
  103.9 9.1 %copy-start.3 = (f32[1792]{0:T(1024)S(1)}, f32[1792]{0:T(1024)}, u32[]{:S(2)}) copy-start(f32[1792]{0:T(1024)} %param.13) | copy-start | bytes 21508
  111.8 1.3 %collective-permute-start.2 = (f32[512,1]{0,1:T(1,128)S(1)}, f32[512,1]{0,1:T(1,128)S(1)}, u32[]{:S(2)}, u32[]{:S(2)}) collective-permute-start(f32[512,1]{0,1:T(1,128)S(1)} %bitcast.25), channel_id=1, source_target_pairs={{0,1},{1,0},{2,3},{3,2},{4,5},{5,4},{6,7},{7,6},{8,9},{9,8},{10,11... | collective-permute-start | bytes 6152 | tf_op jit(solution)/shard_map/ppermute | solution.py:340
